TPU v7x, 256 devices: a whole 4x4x8 slice. The times are simulated.
256 devices in a mesh: rows: 8 (over x_hi, y), cols: 32 (over z, x_lo, core).
Axes of the slice: x: 4 (x_hi: 2, x_lo: 2; x = x_hi * 2 + x_lo), y: 4, z: 8, core: 2. Of those that a mesh axis runs over, the one named last changes fastest.
Arguments:
- features: bfloat16 [4, 256, 64, 4096], P(None, None, 'rows', 'cols'), may hold values from -8 to 8
- cotangent: bfloat16 [4, 256, 64, 4096], P(None, None, 'rows', 'cols'), may hold values from -6 to 6
- reduce_weight: bfloat16 [256, 64], replicated, may hold values from -0.375 to 0.375
- spatial_weight: bfloat16 [9, 64, 64], replicated, may hold values from -0.25 to 0.25
- expand_weight: bfloat16 [64, 256], replicated, may hold values from -0.75 to 0.75
- reduce_factor: float32 [4, 256], replicated, may hold values from 0.25 to 1.75
- spatial_factor: float32 [4, 64], replicated, may hold values from 0.25 to 1.75
- expand_factor: float32 [4, 64], replicated, may hold values from 0.25 to 1.75
- output_factor: float32 [4, 256], replicated, may hold values from 0.25 to 1.75
- gain_first: float32 [64], replicated, may hold values from 0.25 to 1.75
- shift_first: float32 [64], replicated, may hold values from -3 to 3
- gain_second: float32 [64], replicated, may hold values from 0.25 to 1.75
- shift_second: float32 [64], replicated, may hold values from -3 to 3
Outputs:
- grad_features: bfloat16 [4, 256, 64, 4096], P(None, None, 'rows', 'cols')
- grad_reduce: float32 [256, 64], replicated
- grad_spatial: float32 [9, 64, 64], replicated
- grad_expand: float32 [64, 256], replicated
- grad_reduce_factor: float32 [4, 256], replicated
- grad_spatial_factor: float32 [4, 64], replicated
- grad_expand_factor: float32 [4, 64], replicated
- grad_output_factor: float32 [4, 256], replicated
- grad_gain_first: float32 [64], replicated
- grad_shift_first: float32 [64], replicated
- grad_gain_second: float32 [64], replicated
- grad_shift_second: float32 [64], replicated
All inputs are finite; a program needn't handle non-finite values.
Results may differ from a plain program's by a relative error of at most 0.01.
Values may be sent and summed in bfloat16 or wider, within the bound.
A program may use at most 128 MiB of HBM per device.

v0:
```python
import functools
import jax
import jax.numpy as jnp
from jax import lax
from jax.sharding import Mesh
from jax.sharding import PartitionSpec as P

ROWS_COLS = ("rows_0", "rows_1", "cols_0", "cols_1", "cols_2")
ROWS = ("rows_0", "rows_1")
COLS = ("cols_0", "cols_1", "cols_2")
EPSILON = 1e-05


def by_axis(array, axes):
    return functools.reduce(lax.psum, axes, array)


def with_halo(cells, sides, width):
    for axis, dim in sides:
        count = lax.axis_size(axis)
        ends = count - 1
        head = lax.slice_in_dim(cells, 0, width, axis=dim)
        tail = lax.slice_in_dim(cells, cells.shape[dim] - width, cells.shape[dim], axis=dim)
        cells = jnp.concatenate(
            [
                lax.ppermute(tail, axis, [(i, (i + 1) % count) for i in range(ends)]),
                cells,
                lax.ppermute(head, axis, [((i + 1) % count, i) for i in range(ends)]),
            ],
            axis=dim,
        )
    return cells


def packed_total(arrays, axis):
    flat, at, finished = (jnp.concatenate([a.reshape(-1) for a in arrays]), 0, [])
    so_far = lax.psum(flat, axis)
    for a in arrays:
        finished.append(so_far[at : at + a.size].reshape(a.shape))
        at += a.size
    return tuple(finished)


def activate(value):
    return value * jax.nn.sigmoid(value)


def slope(value):
    sig = jax.nn.sigmoid(value)
    return sig * (1.0 + value * (1.0 - sig))


def norm_forward(acts, gain, shift, count):
    total, square = (
        by_axis(jnp.sum(acts, axis=2), ROWS_COLS),
        by_axis(jnp.sum(acts * acts, axis=2), ROWS_COLS),
    )
    mean = total / count
    var = square / count - mean * mean
    centred = acts - mean[:, :, None]
    rstd = lax.rsqrt(var + EPSILON)[:, :, None]
    normed = centred * rstd
    pre = gain[None, :, None] * normed + shift[None, :, None]
    return (activate(pre).astype(jnp.bfloat16), normed, pre, rstd)


def norm_backward(upstream, normed, pre, rstd, gain, count):
    dpre = upstream * slope(pre)
    plain, weighted = (
        by_axis(jnp.sum(dpre, axis=2), ROWS_COLS),
        by_axis(jnp.sum(dpre * normed, axis=2), ROWS_COLS),
    )
    dact = (
        gain[None, :, None]
        * rstd
        * (dpre - plain[:, :, None] / count - normed * weighted[:, :, None] / count)
    )
    return (dact, jnp.sum(weighted, axis=0), jnp.sum(plain, axis=0))


def rim_cells(field):
    return with_halo(field, ((ROWS, 2), (COLS, 3)), 1)


def rim_grads(field):
    return with_halo(field, ((ROWS, 2), (COLS, 3)), 1)


def conv_forward(padded, weights, tall, broad):
    members, narrow = (padded.shape[0], padded.shape[1])
    total = None
    for tap in range(9):
        row_off, col_off = (tap // 3, tap % 3)
        window = padded[:, :, row_off : row_off + tall, col_off : col_off + broad].reshape(
            members, narrow, tall * broad
        )
        term = jnp.einsum(
            "mfo,mfp->mop", weights[:, tap], window, preferred_element_type=jnp.float32
        )
        total = term if total is None else total + term
    return total


def conv_backward(padded_back, padded_one, weights, dact_low, tall, broad):
    members, narrow = (padded_back.shape[0], padded_back.shape[1])
    total = None
    pieces = []
    for tap in range(9):
        row_off, col_off = (tap // 3, tap % 3)
        flipped = padded_back[
            :, :, 2 - row_off : 2 - row_off + tall, 2 - col_off : 2 - col_off + broad
        ].reshape(members, narrow, tall * broad)
        term = jnp.einsum(
            "mfo,mop->mfp", weights[:, tap], flipped, preferred_element_type=jnp.float32
        )
        total = term if total is None else total + term
        window = padded_one[:, :, row_off : row_off + tall, col_off : col_off + broad].reshape(
            members, narrow, tall * broad
        )
        pieces.append(
            jnp.einsum("mfp,mop->mfo", window, dact_low, preferred_element_type=jnp.float32)
        )
    return (total, jnp.stack(pieces, axis=1))


def fold_members(
    part_reduce,
    part_spatial,
    part_expand,
    rw,
    sw,
    ew,
    reduce_factor,
    spatial_factor,
    expand_factor,
    output_factor,
):
    grad_reduce = jnp.sum(part_reduce * reduce_factor[:, :, None], axis=0)
    grad_reduce_factor = jnp.sum(part_reduce * rw[None], axis=2)
    grad_spatial = jnp.sum(part_spatial * spatial_factor[:, None, :, None], axis=0)
    grad_spatial_factor = jnp.sum(part_spatial * sw[None], axis=(1, 3))
    grad_expand = jnp.sum(
        part_expand * expand_factor[:, :, None] * output_factor[:, None, :], axis=0
    )
    grad_expand_factor = jnp.sum(part_expand * ew[None] * output_factor[:, None, :], axis=2)
    grad_output_factor = jnp.sum(part_expand * ew[None] * expand_factor[:, :, None], axis=1)
    return (
        grad_reduce,
        grad_spatial,
        grad_expand,
        grad_reduce_factor,
        grad_spatial_factor,
        grad_expand_factor,
        grad_output_factor,
    )


def body(
    features,
    cotangent,
    reduce_weight,
    spatial_weight,
    expand_weight,
    reduce_factor,
    spatial_factor,
    expand_factor,
    output_factor,
    gain_first,
    shift_first,
    gain_second,
    shift_second,
):
    members, channels, tall, broad = features.shape
    narrow = reduce_weight.shape[1]
    cells = tall * broad
    count = float(cells * lax.axis_size(ROWS) * lax.axis_size(COLS))
    rw = reduce_weight.astype(jnp.float32)
    sw = spatial_weight.astype(jnp.float32)
    ew = expand_weight.astype(jnp.float32)
    member_reduce = (reduce_factor[:, :, None] * rw[None]).astype(jnp.bfloat16)
    member_spatial = (spatial_factor[:, None, :, None] * sw[None]).astype(jnp.bfloat16)
    member_expand = (expand_factor[:, :, None] * ew[None] * output_factor[:, None, :]).astype(
        jnp.bfloat16
    )
    flat = features.reshape(members, channels, cells)
    first = jnp.einsum("mcf,mcp->mfp", member_reduce, flat, preferred_element_type=jnp.float32)
    hidden_one, normed_one, pre_one, rstd_one = norm_forward(first, gain_first, shift_first, count)
    padded_one = rim_cells(hidden_one.reshape(members, narrow, tall, broad))
    second = conv_forward(padded_one, member_spatial, tall, broad)
    hidden_two, normed_two, pre_two, rstd_two = norm_forward(
        second, gain_second, shift_second, count
    )
    third = jnp.einsum(
        "mfc,mfp->mcp", member_expand, hidden_two, preferred_element_type=jnp.float32
    )
    summed = flat.astype(jnp.float32) + third
    upstream = cotangent.reshape(members, channels, cells).astype(jnp.float32) * slope(summed)
    upstream_low = upstream.astype(jnp.bfloat16)
    back_two = jnp.einsum(
        "mfc,mcp->mfp", member_expand, upstream_low, preferred_element_type=jnp.float32
    )
    part_expand = jnp.einsum(
        "mfp,mcp->mfc", hidden_two, upstream_low, preferred_element_type=jnp.float32
    )
    dact_two, grad_gain_second, grad_shift_second = norm_backward(
        back_two, normed_two, pre_two, rstd_two, gain_second, count
    )
    dact_two_low = dact_two.astype(jnp.bfloat16)
    padded_back = rim_grads(dact_two_low.reshape(members, narrow, tall, broad))
    back_one, part_spatial = conv_backward(
        padded_back, padded_one, member_spatial, dact_two_low, tall, broad
    )
    dact_one, grad_gain_first, grad_shift_first = norm_backward(
        back_one, normed_one, pre_one, rstd_one, gain_first, count
    )
    dact_one_low = dact_one.astype(jnp.bfloat16)
    grad_flat = upstream + jnp.einsum(
        "mcf,mfp->mcp", member_reduce, dact_one_low, preferred_element_type=jnp.float32
    )
    grad_features = grad_flat.astype(jnp.bfloat16).reshape(members, channels, tall, broad)
    part_reduce = jnp.einsum("mcp,mfp->mcf", flat, dact_one_low, preferred_element_type=jnp.float32)
    local = fold_members(
        part_reduce,
        part_spatial,
        part_expand,
        rw,
        sw,
        ew,
        reduce_factor,
        spatial_factor,
        expand_factor,
        output_factor,
    )
    totals = packed_total(
        (local[0], local[1], local[2], local[3], local[4], local[5], local[6]), ROWS_COLS
    )
    return (
        grad_features,
        totals[0],
        totals[1],
        totals[2],
        totals[3],
        totals[4],
        totals[5],
        totals[6],
        grad_gain_first,
        grad_shift_first,
        grad_gain_second,
        grad_shift_second,
    )


def solution(mesh):
    split = Mesh(
        mesh.devices.reshape(2, 4, 8, 2, 2), ("rows_0", "rows_1", "cols_0", "cols_1", "cols_2")
    )
    placed = (
        P(None, None, ROWS, COLS),
        P(None, None, ROWS, COLS),
        P(),
        P(),
        P(),
        P(),
        P(),
        P(),
        P(),
        P(),
        P(),
        P(),
        P(),
    )
    return jax.shard_map(
        body,
        mesh=split,
        in_specs=placed,
        out_specs=(
            P(None, None, ROWS, COLS),
            P(),
            P(),
            P(),
            P(),
            P(),
            P(),
            P(),
            P(),
            P(),
            P(),
            P(),
        ),
        check_vma=False,
    )
```

profile of v0, /device:TPU:1, one launch (start us, length us, event | category | flops | bytes accessed | tf_op | source)
XLA Modules:
  0.0 572.1 jit_solution(7597058974139156140)
XLA Ops:
  10.8 5.9 %all-reduce.19 = (f32[4,64]{1,0:T(4,128)S(1)}, f32[4,64]{1,0:T(4,128)S(1)}) all-reduce(f32[4,64]{1,0:T(4,128)S(1)} %get-tuple-element.57, f32[4,64]{1,0:T(4,128)S(1)} %get-tuple-element.56), channel_id=1, replica_groups=mesh['rows_0'=2,'rows_1'=4,'cols_0'=8,'cols_1'=2,'cols_2'=2] {'rows_0'}, use_global_device_ids=true, to_apply=%region_7.0 | all-reduce | flops 512 | bytes 4096 | tf_op jit(solution)/shard_map/psum | solution.py:15
  16.6 8.9 %all-reduce.7 = (f32[4,64]{1,0:T(4,128)S(1)}, f32[4,64]{1,0:T(4,128)S(1)}) all-reduce(f32[4,64]{1,0:T(4,128)S(1)} %get-tuple-element.101, f32[4,64]{1,0:T(4,128)S(1)} %get-tuple-element.102), channel_id=1, replica_groups=mesh['rows_0'=2,'rows_1'=4,'cols_0'=8,'cols_1'=2,'cols_2'=2] {'rows_1'}, use_global_device_ids=true, to_apply=%region_8.0 | all-reduce | flops 512 | bytes 4096 | tf_op jit(solution)/shard_map/psum | solution.py:15
  25.6 16.2 %all-reduce.3 = (f32[4,64]{1,0:T(4,128)S(1)}, f32[4,64]{1,0:T(4,128)S(1)}) all-reduce(f32[4,64]{1,0:T(4,128)S(1)} %get-tuple-element.77, f32[4,64]{1,0:T(4,128)S(1)} %get-tuple-element.78), channel_id=1, replica_groups=mesh['rows_0'=2,'rows_1'=4,'cols_0'=8,'cols_1'=2,'cols_2'=2] {'cols_0'}, use_global_device_ids=true, to_apply=%region_9.0 | all-reduce | flops 512 | bytes 4096 | tf_op jit(solution)/shard_map/psum | solution.py:15
  45.5 10.9 %all-reduce.11 = (f32[4,64]{1,0:T(4,128)S(1)}, f32[4,64]{1,0:T(4,128)S(1)}) all-reduce(f32[4,64]{1,0:T(4,128)S(1)} %get-tuple-element.93, f32[4,64]{1,0:T(4,128)S(1)} %get-tuple-element.94), channel_id=1, replica_groups=mesh['rows_0'=2,'rows_1'=4,'cols_0'=8,'cols_1'=2,'cols_2'=2] {'cols_2'}, use_global_device_ids=true, to_apply=%region_11.0 | all-reduce | flops 512 | bytes 4096 | tf_op jit(solution)/shard_map/psum | solution.py:15
  66.7 4.5 reshape.237
  87.8 5.0 pad_maximum_fusion
  92.9 4.2 fusion.42
  120.8 10.8 %all-reduce.18 = (f32[4,64]{1,0:T(4,128)S(1)}, f32[4,64]{1,0:T(4,128)S(1)}) all-reduce(f32[4,64]{1,0:T(4,128)S(1)} %get-tuple-element.55, f32[4,64]{1,0:T(4,128)S(1)} %get-tuple-element.54), channel_id=1, replica_groups=mesh['rows_0'=2,'rows_1'=4,'cols_0'=8,'cols_1'=2,'cols_2'=2] {'rows_0'}, use_global_device_ids=true, to_apply=%region_19.0 | all-reduce | flops 512 | bytes 4096 | tf_op jit(solution)/shard_map/psum | solution.py:15
  131.7 7.4 %all-reduce.6 = (f32[4,64]{1,0:T(4,128)S(1)}, f32[4,64]{1,0:T(4,128)S(1)}) all-reduce(f32[4,64]{1,0:T(4,128)S(1)} %get-tuple-element.99, f32[4,64]{1,0:T(4,128)S(1)} %get-tuple-element.100), channel_id=1, replica_groups=mesh['rows_0'=2,'rows_1'=4,'cols_0'=8,'cols_1'=2,'cols_2'=2] {'rows_1'}, use_global_device_ids=true, to_apply=%region_20.0 | all-reduce | flops 512 | bytes 4096 | tf_op jit(solution)/shard_map/psum | solution.py:15
  139.1 10.7 %all-reduce.2 = (f32[4,64]{1,0:T(4,128)S(1)}, f32[4,64]{1,0:T(4,128)S(1)}) all-reduce(f32[4,64]{1,0:T(4,128)S(1)} %get-tuple-element.75, f32[4,64]{1,0:T(4,128)S(1)} %get-tuple-element.76), channel_id=1, replica_groups=mesh['rows_0'=2,'rows_1'=4,'cols_0'=8,'cols_1'=2,'cols_2'=2] {'cols_0'}, use_global_device_ids=true, to_apply=%region_21.0 | all-reduce | flops 512 | bytes 4096 | tf_op jit(solution)/shard_map/psum | solution.py:15
  153.5 12.3 %all-reduce.10 = (f32[4,64]{1,0:T(4,128)S(1)}, f32[4,64]{1,0:T(4,128)S(1)}) all-reduce(f32[4,64]{1,0:T(4,128)S(1)} %get-tuple-element.91, f32[4,64]{1,0:T(4,128)S(1)} %get-tuple-element.92), channel_id=1, replica_groups=mesh['rows_0'=2,'rows_1'=4,'cols_0'=8,'cols_1'=2,'cols_2'=2] {'cols_2'}, use_global_device_ids=true, to_apply=%region_23.0 | all-reduce | flops 512 | bytes 4096 | tf_op jit(solution)/shard_map/psum | solution.py:15
  165.9 4.7 multiply_multiply_fusion
  174.6 5.8 %all-reduce.17 = (f32[4,64]{1,0:T(4,128)S(1)}, f32[4,64]{1,0:T(4,128)}) all-reduce(f32[4,64]{1,0:T(4,128)S(1)} %get-tuple-element.53, f32[4,64]{1,0:T(4,128)S(1)} %get-tuple-element.52), channel_id=1, replica_groups=mesh['rows_0'=2,'rows_1'=4,'cols_0'=8,'cols_1'=2,'cols_2'=2] {'rows_0'}, use_global_device_ids=true, to_apply=%region_31.0 | all-reduce | flops 512 | bytes 4096 | tf_op jit(solution)/shard_map/psum | solution.py:15
  180.4 6.1 %all-reduce.5 = (f32[4,64]{1,0:T(4,128)S(1)}, f32[4,64]{1,0:T(4,128)S(1)}) all-reduce(f32[4,64]{1,0:T(4,128)S(1)} %get-tuple-element.97, f32[4,64]{1,0:T(4,128)} %get-tuple-element.98), channel_id=1, replica_groups=mesh['rows_0'=2,'rows_1'=4,'cols_0'=8,'cols_1'=2,'cols_2'=2] {'rows_1'}, use_global_device_ids=true, to_apply=%region_32.0 | all-reduce | flops 512 | bytes 4096 | tf_op jit(solution)/shard_map/psum | solution.py:15
  186.5 13.4 %all-reduce.1 = (f32[4,64]{1,0:T(4,128)S(1)}, f32[4,64]{1,0:T(4,128)}) all-reduce(f32[4,64]{1,0:T(4,128)S(1)} %get-tuple-element.73, f32[4,64]{1,0:T(4,128)S(1)} %get-tuple-element.74), channel_id=1, replica_groups=mesh['rows_0'=2,'rows_1'=4,'cols_0'=8,'cols_1'=2,'cols_2'=2] {'cols_0'}, use_global_device_ids=true, to_apply=%region_33.0 | all-reduce | flops 512 | bytes 4096 | tf_op jit(solution)/shard_map/psum | solution.py:15
  203.8 10.6 %all-reduce.9 = (f32[4,64]{1,0:T(4,128)S(1)}, f32[4,64]{1,0:T(4,128)}) all-reduce(f32[4,64]{1,0:T(4,128)S(1)} %get-tuple-element.89, f32[4,64]{1,0:T(4,128)S(1)} %get-tuple-element.90), channel_id=1, replica_groups=mesh['rows_0'=2,'rows_1'=4,'cols_0'=8,'cols_1'=2,'cols_2'=2] {'cols_2'}, use_global_device_ids=true, to_apply=%region_35.0 | all-reduce | flops 512 | bytes 4096 | tf_op jit(solution)/shard_map/psum | solution.py:15
  226.9 4.3 collective-permute-start.4
  253.6 5.2 maximum_maximum_fusion.1
  268.8 7.9 %all-reduce.16 = (f32[4,64]{1,0:T(4,128)S(1)}, f32[4,64]{1,0:T(4,128)S(1)}) all-reduce(f32[4,64]{1,0:T(4,128)S(1)} %get-tuple-element.51, f32[4,64]{1,0:T(4,128)S(1)} %get-tuple-element.50), channel_id=1, replica_groups=mesh['rows_0'=2,'rows_1'=4,'cols_0'=8,'cols_1'=2,'cols_2'=2] {'rows_0'}, use_global_device_ids=true, to_apply=%region_43.0 | all-reduce | flops 512 | bytes 4096 | tf_op jit(solution)/shard_map/psum | solution.py:15
  276.7 9.6 %all-reduce.4 = (f32[4,64]{1,0:T(4,128)S(1)}, f32[4,64]{1,0:T(4,128)S(1)}) all-reduce(f32[4,64]{1,0:T(4,128)S(1)} %get-tuple-element.95, f32[4,64]{1,0:T(4,128)S(1)} %get-tuple-element.96), channel_id=1, replica_groups=mesh['rows_0'=2,'rows_1'=4,'cols_0'=8,'cols_1'=2,'cols_2'=2] {'rows_1'}, use_global_device_ids=true, to_apply=%region_44.0 | all-reduce | flops 512 | bytes 4096 | tf_op jit(solution)/shard_map/psum | solution.py:15
  286.2 10.8 %all-reduce = (f32[4,64]{1,0:T(4,128)S(1)}, f32[4,64]{1,0:T(4,128)S(1)}) all-reduce(f32[4,64]{1,0:T(4,128)S(1)} %get-tuple-element.71, f32[4,64]{1,0:T(4,128)S(1)} %get-tuple-element.72), channel_id=1, replica_groups=mesh['rows_0'=2,'rows_1'=4,'cols_0'=8,'cols_1'=2,'cols_2'=2] {'cols_0'}, use_global_device_ids=true, to_apply=%region_45.0 | all-reduce | flops 512 | bytes 4096 | tf_op jit(solution)/shard_map/psum | solution.py:15
  297.0 5.1 all-reduce.12
  302.1 8.7 %all-reduce.8 = (f32[4,64]{1,0:T(4,128)S(1)}, f32[4,64]{1,0:T(4,128)S(1)}) all-reduce(f32[4,64]{1,0:T(4,128)S(1)} %get-tuple-element.87, f32[4,64]{1,0:T(4,128)S(1)} %get-tuple-element.88), channel_id=1, replica_groups=mesh['rows_0'=2,'rows_1'=4,'cols_0'=8,'cols_1'=2,'cols_2'=2] {'cols_2'}, use_global_device_ids=true, to_apply=%region_47.0 | all-reduce | flops 512 | bytes 4096 | tf_op jit(solution)/shard_map/psum | solution.py:15
  320.3 236.9 %all-reduce.22.cloned.1.call-done = f32[72192]{0:T(1024)} async-done(((f32[72192]{0:T(1024)}), f32[72192]{0:T(1024)}) %all-reduce.22.cloned.1.call-update) | async-done | bytes 288784 | tf_op jit(solution)/shard_map/psum | solution.py:37
  (220 shorter events, 131.3 us)
Async XLA Ops:
  7.2 550.0 %all-reduce.22.cloned.1.call-start = ((), (), s32[]{:S(2)}) async-start(), calls=%async_computation | async-start | bytes 581632 | tf_op jit(solution)/shard_map/psum | solution.py:37
  10.1 46.3 %copy-start.39 = (f32[64]{0:T(128)S(1)}, f32[64]{0:T(128)}, u32[]{:S(2)}) copy-start(f32[64]{0:T(128)} %param.22) | copy-start | bytes 772
  10.1 46.3 %copy-start.42 = (f32[64]{0:T(128)S(1)}, f32[64]{0:T(128)}, u32[]{:S(2)}) copy-start(f32[64]{0:T(128)} %param.23) | copy-start | bytes 772
  10.7 47.4 %copy-start = (f32[4,64,1024]{2,1,0:T(8,128)}, f32[4,64,1024]{2,1,0:T(8,128)S(1)}, u32[]{:S(2)}) copy-start(f32[4,64,1024]{2,1,0:T(8,128)S(1)} %get-tuple-element.147) | copy-start | bytes 3145732
  58.2 6.9 %copy-start.38 = (f32[4,64]{1,0:T(4,128)S(1)}, f32[4,64]{1,0:T(4,128)}, u32[]{:S(2)}) copy-start(f32[4,64]{1,0:T(4,128)} %param.19) | copy-start | bytes 3076
  60.0 6.0 %copy-start.37 = (bf16[64,256]{1,0:T(8,128)(2,1)S(1)}, bf16[64,256]{1,0:T(8,128)(2,1)}, u32[]{:S(2)}) copy-start(bf16[64,256]{1,0:T(8,128)(2,1)} %param.17) | copy-start | bytes 98308
  60.8 10.4 %collective-permute-start = (bf16[4,64,1,128]{1,0,3,2:T(4,128)(2,1)}, bf16[4,64,1,128]{1,0,3,2:T(4,128)(2,1)}, u32[]{:S(2)}, u32[]{:S(2)}) collective-permute-start(bf16[4,64,1,128]{1,0,3,2:T(4,128)(2,1)} %get-tuple-element.125), channel_id=1, source_target_pairs={{0,32},{32,64},{64,96},{96,128},{128,160},{160,192},{192,224},{1,3... | collective-permute-start | bytes 196616 | tf_op jit(solution)/shard_map/ppermute | solution.py:26
  62.8 8.5 %collective-permute-start.1 = (bf16[4,64,1,128]{1,0,3,2:T(4,128)(2,1)}, bf16[4,64,1,128]{1,0,3,2:T(4,128)(2,1)}, u32[]{:S(2)}, u32[]{:S(2)}) collective-permute-start(bf16[4,64,1,128]{1,0,3,2:T(4,128)(2,1)} %get-tuple-element.126), channel_id=1, source_target_pairs={{32,0},{64,32},{96,64},{128,96},{160,128},{192,160},{224,192},{33,... | collective-permute-start | bytes 196616 | tf_op jit(solution)/shard_map/ppermute | solution.py:28
  71.9 15.9 %collective-permute-start.2 = (bf16[4,64,10,1]{1,0,3,2:T(4,128)(2,1)S(1)}, bf16[4,64,10,1]{1,0,3,2:T(4,128)(2,1)S(1)}, u32[]{:S(2)}, u32[]{:S(2)}) collective-permute-start(bf16[4,64,10,1]{1,0,3,2:T(4,128)(2,1)S(1)} %get-tuple-element.122), channel_id=1, source_target_pairs={{0,1},{1,2},{2,3},{3,4},{4,5},{5,6},{6,7},{7,8},{8,9},{9,10},{10,1... | collective-permute-start | bytes 15368 | tf_op jit(solution)/shard_map/ppermute | solution.py:26
  75.5 12.4 %collective-permute-start.3 = (bf16[4,64,10,1]{1,0,3,2:T(4,128)(2,1)S(1)}, bf16[4,64,10,1]{1,0,3,2:T(4,128)(2,1)S(1)}, u32[]{:S(2)}, u32[]{:S(2)}) collective-permute-start(bf16[4,64,10,1]{1,0,3,2:T(4,128)(2,1)S(1)} %get-tuple-element.121), channel_id=1, source_target_pairs={{1,0},{2,1},{3,2},{4,3},{5,4},{6,5},{7,6},{8,7},{9,8},{10,9},{11,1... | collective-permute-start | bytes 15368 | tf_op jit(solution)/shard_map/ppermute | solution.py:28
  98.7 4.8 copy-start.6
  98.7 4.8 copy-start.4
  119.6 46.2 %copy-start.44 = (f32[64]{0:T(128)S(1)}, f32[64]{0:T(128)}, u32[]{:S(2)}) copy-start(f32[64]{0:T(128)} %param.24) | copy-start | bytes 772
  165.8 4.7 copy-start.24
  165.8 4.7 copy-start.33
  165.8 4.7 copy-start.45
  165.8 4.7 copy-start.46
  165.8 4.7 copy-start.47
  226.1 8.8 %copy-start.34 = (f32[64,256]{1,0:T(8,128)S(1)}, f32[64,256]{1,0:T(8,128)}, u32[]{:S(2)}) copy-start(f32[64,256]{1,0:T(8,128)} %get-tuple-element.60) | copy-start | bytes 196612
  226.9 10.6 %collective-permute-start.4 = (bf16[4,64,1,128]{1,0,3,2:T(4,128)(2,1)}, bf16[4,64,1,128]{1,0,3,2:T(4,128)(2,1)}, u32[]{:S(2)}, u32[]{:S(2)}) collective-permute-start(bf16[4,64,1,128]{1,0,3,2:T(4,128)(2,1)} %get-tuple-element.123), channel_id=1, source_target_pairs={{0,32},{32,64},{64,96},{96,128},{128,160},{160,192},{192,224},{1,3... | collective-permute-start | bytes 196616 | tf_op jit(solution)/shard_map/ppermute | solution.py:26
  231.2 5.7 copy-start.41
  231.2 6.8 %collective-permute-start.5 = (bf16[4,64,1,128]{1,0,3,2:T(4,128)(2,1)}, bf16[4,64,1,128]{1,0,3,2:T(4,128)(2,1)}, u32[]{:S(2)}, u32[]{:S(2)}) collective-permute-start(bf16[4,64,1,128]{1,0,3,2:T(4,128)(2,1)} %get-tuple-element.124), channel_id=1, source_target_pairs={{32,0},{64,32},{96,64},{128,96},{160,128},{192,160},{224,192},{33,... | collective-permute-start | bytes 196616 | tf_op jit(solution)/shard_map/ppermute | solution.py:28
  238.7 15.0 %collective-permute-start.6 = (bf16[4,64,10,1]{1,0,3,2:T(4,128)(2,1)S(1)}, bf16[4,64,10,1]{1,0,3,2:T(4,128)(2,1)S(1)}, u32[]{:S(2)}, u32[]{:S(2)}) collective-permute-start(bf16[4,64,10,1]{1,0,3,2:T(4,128)(2,1)S(1)} %get-tuple-element.118), channel_id=1, source_target_pairs={{1,0},{2,1},{3,2},{4,3},{5,4},{6,5},{7,6},{8,7},{9,8},{10,9},{11,1... | collective-permute-start | bytes 15368 | tf_op jit(solution)/shard_map/ppermute | solution.py:28
  242.1 11.6 %collective-permute-start.7 = (bf16[4,64,10,1]{1,0,3,2:T(4,128)(2,1)S(1)}, bf16[4,64,10,1]{1,0,3,2:T(4,128)(2,1)S(1)}, u32[]{:S(2)}, u32[]{:S(2)}) collective-permute-start(bf16[4,64,10,1]{1,0,3,2:T(4,128)(2,1)S(1)} %get-tuple-element.117), channel_id=1, source_target_pairs={{0,1},{1,2},{2,3},{3,4},{4,5},{5,6},{6,7},{7,8},{8,9},{9,10},{10,1... | collective-permute-start | bytes 15368 | tf_op jit(solution)/shard_map/ppermute | solution.py:26
  (34 other events, 49.5 us)
Sparse Core Ops, SparseCore 0:
  315.0 242.1 all-reduce.21
where the time goes:
time: 575 us; the launch traced here: 572 us
  waiting for transfers between devices  237 us (41%)
  blocking collectives  172 us (30%)
  local copies, waits for them, and re-layouts  71 us (12%)
  other arithmetic  28.2 us (5%)
  matrix products  28 us (5%)
  starting transfers between devices  20.1 us (3%)
  between operations  14.9 us (3%)
    psum x1, waiting for transfers between devices, packed_total(): so_far = lax.psum(flat, axis)  237 us
    psum x20, blocking collectives, by_axis(): return functools.reduce(lax.psum, axes, array)  172 us
    reshape x8, local copies, waits for them, and re-layouts, conv_forward(): padded[:, :, row_off:row_off + tall, col_off:col_off + broad]  17.3 us
    concatenate x6, other arithmetic, with_halo(): jnp.concatenate([lax.ppermute(tail, axis, [(i, (i + 1) % count) for i in...  17.3 us
    unnamed x111, local copies, waits for them, and re-layouts  13.8 us
    ppermute x4, starting transfers between devices, with_halo(): lax.ppermute(tail, axis, [(i, (i + 1) % count) for i in range(ends)])  12.1 us
  transfers between devices with their start and end apart: 9, of which 2 were waited for; matrix products, arithmetic and copies ran while one was open for 6% of the time, Pallas kernels for 0%

commit v1 on v0

--- a/solution.py
+++ b/solution.py
@@ -34,7 +34,7 @@
 
 def packed_total(arrays, axis):
     flat, at, finished = (jnp.concatenate([a.reshape(-1) for a in arrays]), 0, [])
-    so_far = lax.psum(flat, axis)
+    so_far = jnp.sum(lax.all_gather(flat, axis), axis=0)
     for a in arrays:
         finished.append(so_far[at : at + a.size].reshape(a.shape))
         at += a.size

time: 575 us -> 860 us (1.50)
  waiting for transfers between devices: 237 us -> 472 us
  other arithmetic: 28.2 us -> 78.8 us
    all_gather x0 -> x1, waiting for transfers between devices: none -> 472 us  [packed_total(): so_far = jnp.sum(lax.all_gather(flat, axis), axis=0)]
    psum x1 -> x0, waiting for transfers between devices: 237 us -> none  [packed_total(): so_far = lax.psum(flat, axis)]
    reduce_sum x0 -> x1, other arithmetic: none -> 49.7 us  [packed_total(): so_far = jnp.sum(lax.all_gather(flat, axis), axis=0)]
  transfers between devices with their start and end apart: 9 -> 9, of which waited for: 2 -> 1; matrix products, arithmetic and copies ran while one was open for 6% -> 4% of each run, Pallas kernels for 0% -> 0%
where the time goes in v1:
time: 860 us; the launch traced here: 857 us
  waiting for transfers between devices  472 us (55%)
  blocking collectives  175 us (20%)
  other arithmetic  78.8 us (9%)
  local copies, waits for them, and re-layouts  70.8 us (8%)
  matrix products  25.5 us (3%)
  starting transfers between devices  20 us (2%)
  between operations  14.9 us (2%)
    all_gather x1, waiting for transfers between devices, packed_total(): so_far = jnp.sum(lax.all_gather(flat, axis), axis=0)  472 us
    psum x20, blocking collectives, by_axis(): return functools.reduce(lax.psum, axes, array)  175 us
    reduce_sum x1, other arithmetic, packed_total(): so_far = jnp.sum(lax.all_gather(flat, axis), axis=0)  49.7 us
    concatenate x6, other arithmetic, with_halo(): jnp.concatenate([lax.ppermute(tail, axis, [(i, (i + 1) % count) for i in...  17.4 us
  transfers between devices with their start and end apart: 9, of which 1 were waited for; matrix products, arithmetic and copies ran while one was open for 4% of the time, Pallas kernels for 0%

profile of v1, /device:TPU:1, one launch (start us, length us, event | category | flops | bytes accessed | tf_op | source)
XLA Modules:
  0.0 856.6 jit_solution(6580595784243290432)
XLA Ops:
  11.5 5.9 all-reduce.19
  17.4 8.9 %all-reduce.7 = (f32[4,64]{1,0:T(4,128)S(1)}, f32[4,64]{1,0:T(4,128)S(1)}) all-reduce(f32[4,64]{1,0:T(4,128)S(1)} %get-tuple-element.101, f32[4,64]{1,0:T(4,128)S(1)} %get-tuple-element.102), channel_id=1, replica_groups=mesh['rows_0'=2,'rows_1'=4,'cols_0'=8,'cols_1'=2,'cols_2'=2] {'rows_1'}, use_global_device_ids=true, to_apply=%region_8.0 | all-reduce | flops 512 | bytes 4096 | tf_op jit(solution)/shard_map/psum | solution.py:15
  26.3 16.2 %all-reduce.3 = (f32[4,64]{1,0:T(4,128)S(1)}, f32[4,64]{1,0:T(4,128)S(1)}) all-reduce(f32[4,64]{1,0:T(4,128)S(1)} %get-tuple-element.77, f32[4,64]{1,0:T(4,128)S(1)} %get-tuple-element.78), channel_id=1, replica_groups=mesh['rows_0'=2,'rows_1'=4,'cols_0'=8,'cols_1'=2,'cols_2'=2] {'cols_0'}, use_global_device_ids=true, to_apply=%region_9.0 | all-reduce | flops 512 | bytes 4096 | tf_op jit(solution)/shard_map/psum | solution.py:15
  46.3 10.9 %all-reduce.11 = (f32[4,64]{1,0:T(4,128)S(1)}, f32[4,64]{1,0:T(4,128)S(1)}) all-reduce(f32[4,64]{1,0:T(4,128)S(1)} %get-tuple-element.93, f32[4,64]{1,0:T(4,128)S(1)} %get-tuple-element.94), channel_id=1, replica_groups=mesh['rows_0'=2,'rows_1'=4,'cols_0'=8,'cols_1'=2,'cols_2'=2] {'cols_2'}, use_global_device_ids=true, to_apply=%region_11.0 | all-reduce | flops 512 | bytes 4096 | tf_op jit(solution)/shard_map/psum | solution.py:15
  67.5 4.5 reshape.237
  88.8 5.0 pad_maximum_fusion
  119.7 10.9 %all-reduce.18 = (f32[4,64]{1,0:T(4,128)S(1)}, f32[4,64]{1,0:T(4,128)S(1)}) all-reduce(f32[4,64]{1,0:T(4,128)S(1)} %get-tuple-element.55, f32[4,64]{1,0:T(4,128)S(1)} %get-tuple-element.54), channel_id=1, replica_groups=mesh['rows_0'=2,'rows_1'=4,'cols_0'=8,'cols_1'=2,'cols_2'=2] {'rows_0'}, use_global_device_ids=true, to_apply=%region_19.0 | all-reduce | flops 512 | bytes 4096 | tf_op jit(solution)/shard_map/psum | solution.py:15
  130.6 7.3 all-reduce.6
  137.9 11.0 %all-reduce.2 = (f32[4,64]{1,0:T(4,128)S(1)}, f32[4,64]{1,0:T(4,128)S(1)}) all-reduce(f32[4,64]{1,0:T(4,128)S(1)} %get-tuple-element.75, f32[4,64]{1,0:T(4,128)S(1)} %get-tuple-element.76), channel_id=1, replica_groups=mesh['rows_0'=2,'rows_1'=4,'cols_0'=8,'cols_1'=2,'cols_2'=2] {'cols_0'}, use_global_device_ids=true, to_apply=%region_21.0 | all-reduce | flops 512 | bytes 4096 | tf_op jit(solution)/shard_map/psum | solution.py:15
  152.9 9.9 %all-reduce.10 = (f32[4,64]{1,0:T(4,128)S(1)}, f32[4,64]{1,0:T(4,128)S(1)}) all-reduce(f32[4,64]{1,0:T(4,128)S(1)} %get-tuple-element.91, f32[4,64]{1,0:T(4,128)S(1)} %get-tuple-element.92), channel_id=1, replica_groups=mesh['rows_0'=2,'rows_1'=4,'cols_0'=8,'cols_1'=2,'cols_2'=2] {'cols_2'}, use_global_device_ids=true, to_apply=%region_23.0 | all-reduce | flops 512 | bytes 4096 | tf_op jit(solution)/shard_map/psum | solution.py:15
  162.9 4.7 multiply_multiply_fusion
  171.6 5.8 all-reduce.17
  177.5 6.7 all-reduce.5
  184.1 12.4 %all-reduce.1 = (f32[4,64]{1,0:T(4,128)}, f32[4,64]{1,0:T(4,128)}) all-reduce(f32[4,64]{1,0:T(4,128)S(1)} %get-tuple-element.73, f32[4,64]{1,0:T(4,128)S(1)} %get-tuple-element.74), channel_id=1, replica_groups=mesh['rows_0'=2,'rows_1'=4,'cols_0'=8,'cols_1'=2,'cols_2'=2] {'cols_0'}, use_global_device_ids=true, to_apply=%region_33.0 | all-reduce | flops 512 | bytes 4096 | tf_op jit(solution)/shard_map/psum | solution.py:15
  196.5 4.5 all-reduce.13
  201.0 10.8 %all-reduce.9 = (f32[4,64]{1,0:T(4,128)S(1)}, f32[4,64]{1,0:T(4,128)}) all-reduce(f32[4,64]{1,0:T(4,128)S(1)} %get-tuple-element.89, f32[4,64]{1,0:T(4,128)} %get-tuple-element.90), channel_id=1, replica_groups=mesh['rows_0'=2,'rows_1'=4,'cols_0'=8,'cols_1'=2,'cols_2'=2] {'cols_2'}, use_global_device_ids=true, to_apply=%region_35.0 | all-reduce | flops 512 | bytes 4096 | tf_op jit(solution)/shard_map/psum | solution.py:15
  225.0 4.3 collective-permute-start.4
  251.6 5.3 maximum_maximum_fusion.1
  267.2 8.4 all-reduce.16
  275.7 9.1 %all-reduce.4 = (f32[4,64]{1,0:T(4,128)S(1)}, f32[4,64]{1,0:T(4,128)S(1)}) all-reduce(f32[4,64]{1,0:T(4,128)S(1)} %get-tuple-element.95, f32[4,64]{1,0:T(4,128)S(1)} %get-tuple-element.96), channel_id=1, replica_groups=mesh['rows_0'=2,'rows_1'=4,'cols_0'=8,'cols_1'=2,'cols_2'=2] {'rows_1'}, use_global_device_ids=true, to_apply=%region_44.0 | all-reduce | flops 512 | bytes 4096 | tf_op jit(solution)/shard_map/psum | solution.py:15
  284.8 11.5 %all-reduce = (f32[4,64]{1,0:T(4,128)S(1)}, f32[4,64]{1,0:T(4,128)S(1)}) all-reduce(f32[4,64]{1,0:T(4,128)S(1)} %get-tuple-element.71, f32[4,64]{1,0:T(4,128)S(1)} %get-tuple-element.72), channel_id=1, replica_groups=mesh['rows_0'=2,'rows_1'=4,'cols_0'=8,'cols_1'=2,'cols_2'=2] {'cols_0'}, use_global_device_ids=true, to_apply=%region_45.0 | all-reduce | flops 512 | bytes 4096 | tf_op jit(solution)/shard_map/psum | solution.py:15
  300.1 12.8 %all-reduce.8 = (f32[4,64]{1,0:T(4,128)S(1)}, f32[4,64]{1,0:T(4,128)S(1)}) all-reduce(f32[4,64]{1,0:T(4,128)S(1)} %get-tuple-element.87, f32[4,64]{1,0:T(4,128)S(1)} %get-tuple-element.88), channel_id=1, replica_groups=mesh['rows_0'=2,'rows_1'=4,'cols_0'=8,'cols_1'=2,'cols_2'=2] {'cols_2'}, use_global_device_ids=true, to_apply=%region_47.0 | all-reduce | flops 512 | bytes 4096 | tf_op jit(solution)/shard_map/psum | solution.py:15
  323.1 472.0 %all-gather.4.cloned.1.call-done = f32[256,1,72192]{2,1,0:T(1,128)} async-done(((f32[1,1,72192]{2,1,0:T(1,128)}), f32[256,1,72192]{2,1,0:T(1,128)}) %all-gather.4.cloned.1.call-update) | async-done | bytes 73924624 | tf_op jit(solution)/shard_map/all_gather | solution.py:37
  795.1 49.7 %reduce_sum.195 = f32[72192]{0:T(1024)S(1)} reduce(f32[256,1,72192]{2,1,0:T(1,128)} %all-gather.4.cloned.1.call-done, f32[]{:T(128)} %constant.16.clone.1), dimensions={0,1}, to_apply=%region_55.0 | reduce | flops 18408960 | bytes 74213376 | tf_op jit(solution)/shard_map/reduce_sum | solution.py:37
  (222 shorter events, 133.2 us)
Async XLA Ops:
  7.2 787.9 %all-gather.4.cloned.1.call-start = ((), (), s32[]{:S(2)}) async-start(), calls=%async_computation | async-start | bytes 74213376 | tf_op jit(solution)/shard_map/all_gather | solution.py:37
  10.9 46.3 %copy-start.40 = (f32[64]{0:T(128)S(1)}, f32[64]{0:T(128)}, u32[]{:S(2)}) copy-start(f32[64]{0:T(128)} %param.22) | copy-start | bytes 772
  10.9 46.3 %copy-start.42 = (f32[64]{0:T(128)S(1)}, f32[64]{0:T(128)}, u32[]{:S(2)}) copy-start(f32[64]{0:T(128)} %param.23) | copy-start | bytes 772
  11.5 47.4 %copy-start = (f32[4,64,1024]{2,1,0:T(8,128)}, f32[4,64,1024]{2,1,0:T(8,128)S(1)}, u32[]{:S(2)}) copy-start(f32[4,64,1024]{2,1,0:T(8,128)S(1)} %get-tuple-element.147) | copy-start | bytes 3145732
  58.9 6.9 copy-start.37
  60.8 6.0 copy-start.36
  61.6 10.4 %collective-permute-start = (bf16[4,64,1,128]{1,0,3,2:T(4,128)(2,1)}, bf16[4,64,1,128]{1,0,3,2:T(4,128)(2,1)}, u32[]{:S(2)}, u32[]{:S(2)}) collective-permute-start(bf16[4,64,1,128]{1,0,3,2:T(4,128)(2,1)} %get-tuple-element.125), channel_id=1, source_target_pairs={{0,32},{32,64},{64,96},{96,128},{128,160},{160,192},{192,224},{1,3... | collective-permute-start | bytes 196616 | tf_op jit(solution)/shard_map/ppermute | solution.py:26
  63.5 8.4 collective-permute-start.1
  72.7 16.1 %collective-permute-start.3 = (bf16[4,64,10,1]{1,0,3,2:T(4,128)(2,1)S(1)}, bf16[4,64,10,1]{1,0,3,2:T(4,128)(2,1)S(1)}, u32[]{:S(2)}, u32[]{:S(2)}) collective-permute-start(bf16[4,64,10,1]{1,0,3,2:T(4,128)(2,1)S(1)} %get-tuple-element.121), channel_id=1, source_target_pairs={{1,0},{2,1},{3,2},{4,3},{5,4},{6,5},{7,6},{8,7},{9,8},{10,9},{11,1... | collective-permute-start | bytes 15368 | tf_op jit(solution)/shard_map/ppermute | solution.py:28
  75.1 13.7 %collective-permute-start.2 = (bf16[4,64,10,1]{1,0,3,2:T(4,128)(2,1)S(1)}, bf16[4,64,10,1]{1,0,3,2:T(4,128)(2,1)S(1)}, u32[]{:S(2)}, u32[]{:S(2)}) collective-permute-start(bf16[4,64,10,1]{1,0,3,2:T(4,128)(2,1)S(1)} %get-tuple-element.122), channel_id=1, source_target_pairs={{0,1},{1,2},{2,3},{3,4},{4,5},{5,6},{6,7},{7,8},{8,9},{9,10},{10,1... | collective-permute-start | bytes 15368 | tf_op jit(solution)/shard_map/ppermute | solution.py:26
  105.3 4.8 copy-start.6
  105.3 4.8 copy-start.4
  118.5 44.4 %copy-start.44 = (f32[64]{0:T(128)S(1)}, f32[64]{0:T(128)}, u32[]{:S(2)}) copy-start(f32[64]{0:T(128)} %param.24) | copy-start | bytes 772
  162.9 4.7 copy-start.25
  162.9 4.7 copy-start.33
  162.9 4.7 copy-start.46
  162.9 4.7 copy-start.47
  162.9 4.7 copy-start.48
  211.7 3.2 copy-start.7
  224.2 9.3 %copy-start.34 = (f32[64,256]{1,0:T(8,128)S(1)}, f32[64,256]{1,0:T(8,128)}, u32[]{:S(2)}) copy-start(f32[64,256]{1,0:T(8,128)} %get-tuple-element.60) | copy-start | bytes 196612
  225.0 11.0 %collective-permute-start.4 = (bf16[4,64,1,128]{1,0,3,2:T(4,128)(2,1)}, bf16[4,64,1,128]{1,0,3,2:T(4,128)(2,1)}, u32[]{:S(2)}, u32[]{:S(2)}) collective-permute-start(bf16[4,64,1,128]{1,0,3,2:T(4,128)(2,1)} %get-tuple-element.123), channel_id=1, source_target_pairs={{0,32},{32,64},{64,96},{96,128},{128,160},{160,192},{192,224},{1,3... | collective-permute-start | bytes 196616 | tf_op jit(solution)/shard_map/ppermute | solution.py:26
  229.3 6.8 collective-permute-start.5
  236.8 14.8 %collective-permute-start.7 = (bf16[4,64,10,1]{1,0,3,2:T(4,128)(2,1)S(1)}, bf16[4,64,10,1]{1,0,3,2:T(4,128)(2,1)S(1)}, u32[]{:S(2)}, u32[]{:S(2)}) collective-permute-start(bf16[4,64,10,1]{1,0,3,2:T(4,128)(2,1)S(1)} %get-tuple-element.117), channel_id=1, source_target_pairs={{0,1},{1,2},{2,3},{3,4},{4,5},{5,6},{6,7},{7,8},{8,9},{9,10},{10,1... | collective-permute-start | bytes 15368 | tf_op jit(solution)/shard_map/ppermute | solution.py:26
  240.3 11.3 %collective-permute-start.6 = (bf16[4,64,10,1]{1,0,3,2:T(4,128)(2,1)S(1)}, bf16[4,64,10,1]{1,0,3,2:T(4,128)(2,1)S(1)}, u32[]{:S(2)}, u32[]{:S(2)}) collective-permute-start(bf16[4,64,10,1]{1,0,3,2:T(4,128)(2,1)S(1)} %get-tuple-element.118), channel_id=1, source_target_pairs={{1,0},{2,1},{3,2},{4,3},{5,4},{6,5},{7,6},{8,7},{9,8},{10,9},{11,1... | collective-permute-start | bytes 15368 | tf_op jit(solution)/shard_map/ppermute | solution.py:28
  (34 other events, 45.7 us)
Sparse Core Ops, SparseCore 0:
  317.3 477.8 all-gather.3
